TPU v7x, 32 devices: a whole 2x2x4 slice. The times are simulated.
32 devices in a mesh: dp: 8 (over y, x, core), mp: 4 (over z).
Axes of the slice: x: 2, y: 2, z: 4, core: 2. Of those that a mesh axis runs over, the one named last changes fastest.
Arguments:
- train_acts: bfloat16 [4096, 2560], P('dp'), may hold values from -6 to 6
- train_grads: bfloat16 [4096, 2560], P('dp'), may hold values from -6 to 6
- lengths: int32 [32], P('dp'), may hold values from 1 to 256, as said below
- query_acts: bfloat16 [128, 2560], replicated, may hold values from -6 to 6
- query_grads: bfloat16 [128, 2560], replicated, may hold values from -0.0059814453 to 0.0059814453
- basis_in: bfloat16 [2560, 2560], P(None, 'mp'), may hold values from -0.125 to 0.125
- basis_out: bfloat16 [2560, 2560], P(None, 'mp'), may hold values from -0.125 to 0.125
Outputs:
- scores: float32 [1, 32], P(None, 'dp')
Inputs may be any that keep to these rules, and one draw needn't show every extreme that they name: The 4 lengths of one index of dp sum to at most 512; in every draw some index's sequences fill all 512 rows and one of them has exactly 256 tokens.
All inputs are finite; a program needn't handle non-finite values.
Results may differ from a plain program's by a relative error of at most 0.0045.
Values may be sent and summed in bfloat16 or wider, within the bound.
A program may use at most 128 MiB of HBM per device.

v0:
```python
import jax
import jax.numpy as jnp
from jax import lax
from jax.sharding import PartitionSpec as P

QUERIES = 1
QLEN = 128


damping_ratio = 0.1


def rotate(values, basis):
    return jnp.dot(values, basis, preferred_element_type=jnp.float32).astype(jnp.bfloat16)


def shards(train_acts, train_grads, lengths, query_acts, query_grads, basis_in, basis_out):
    capacity = train_acts.shape[0]
    window = capacity // 2
    slot_count = lengths.shape[0]
    acts_block = rotate(train_acts, basis_in)
    query_block = rotate(query_acts, basis_in)
    acts_rot, query_rot = (
        lax.all_gather(acts_block, "mp", axis=1, tiled=True),
        lax.all_gather(query_block, "mp", axis=1, tiled=True),
    )
    grads_rot = rotate(train_grads, basis_out)
    query_grot = rotate(query_grads, basis_out).reshape(QUERIES, QLEN, -1)
    finish = jnp.cumsum(lengths)
    starts = finish - lengths
    position = jnp.arange(window, dtype=jnp.int32)
    curvature_local = jnp.zeros((grads_rot.shape[1], acts_rot.shape[1]), jnp.float32)
    stored_list = []
    for slot in range(slot_count):
        begin = jnp.minimum(starts[slot], capacity - window)
        grads_win = lax.dynamic_slice_in_dim(grads_rot, begin, window, 0)
        acts_win = lax.dynamic_slice_in_dim(acts_rot, begin, window, 0)
        inside = (position + begin >= starts[slot]) & (position + begin < finish[slot])
        grads_win = jnp.where(inside[:, None], grads_win, jnp.zeros_like(grads_win))
        product = lax.dot_general(
            grads_win, acts_win, (((0,), (0,)), ((), ())), preferred_element_type=jnp.float32
        )
        curvature_local = curvature_local + product * product
        stored_list.append(product.astype(jnp.bfloat16))
    stored = jnp.stack(stored_list)
    inverse_count = 1.0 / (slot_count * lax.axis_size("dp"))
    query_full = query_rot.reshape(QUERIES, QLEN, -1)
    curvature = lax.psum(curvature_local, "dp") * inverse_count
    grand_total = lax.psum(jnp.sum(curvature), "mp")
    damping = damping_ratio * grand_total / (curvature.size * lax.axis_size("mp"))
    local_grad = jnp.einsum(
        "qti,qtj->qij", query_grot, query_full, preferred_element_type=jnp.float32
    )
    precond = (local_grad / (curvature + damping)).astype(jnp.bfloat16)
    partial_value = jnp.einsum("qik,sik->qs", precond, stored, preferred_element_type=jnp.float32)
    return lax.psum(partial_value, "mp")


def solution(mesh):
    return jax.shard_map(
        shards,
        mesh=mesh,
        in_specs=(P("dp", None), P("dp", None), P("dp"), P(), P(), P(None, "mp"), P(None, "mp")),
        out_specs=P(None, "dp"),
        check_vma=False,
    )
```

profile of v0, /device:TPU:0, one launch (start us, length us, event | category | flops | bytes accessed | tf_op | source)
XLA Modules:
  0.0 276.5 jit_solution(13242700860598171906)
XLA Ops:
  6.5 0.0 copy-start
  6.5 0.0 copy-start.5
  6.5 0.0 all-gather.2.cloned.1.call-start
  6.5 5.9 %convolution_convert_fusion = bf16[512,640]{1,0:T(8,128)(2,1)} fusion(bf16[512,2560]{1,0:T(8,128)(2,1)} %param.7, bf16[2560,640]{1,0:T(8,128)(2,1)} %param.12), kind=kOutput, calls=%fused_computation.12 | convolution fusion | flops 1678049280 | bytes 6553600 | tf_op jit(solution)/shard_map/dot_general | solution.py:14
  12.4 0.0 all-gather.2.cloned.1.call-update
  12.5 0.0 all-reduce.2.cloned.1.call-start
  12.5 0.0 copy-done.5
  12.5 0.2 reduce-window.4
  12.7 0.6 fusion.42
  15.9 0.6 fusion.41
  16.5 1.2 compare_and_fusion.1
  17.7 1.3 compare_and_fusion.2
  19.0 1.3 compare_and_fusion
  20.2 1.3 compare_and_fusion.3
  21.5 0.0 copy-done
  21.5 5.0 %convolution_convert_fusion.1 = bf16[512,640]{1,0:T(8,128)(2,1)} fusion(bf16[512,2560]{1,0:T(8,128)(2,1)} %param.8, bf16[2560,640]{1,0:T(8,128)(2,1)S(1)} %copy-done), kind=kOutput, calls=%fused_computation.13 | convolution fusion | flops 1678049280 | bytes 6553600 | tf_op jit(solution)/shard_map/dot_general | solution.py:14
  26.5 43.4 %all-gather.2.cloned.1.call-done = bf16[512,2560]{1,0:T(8,128)(2,1)} async-done(((bf16[512,640]{1,0:T(8,128)(2,1)}), bf16[512,2560]{1,0:T(8,128)(2,1)}) %all-gather.2.cloned.1.call-update) | async-done | bytes 2621456 | tf_op jit(solution)/shard_map/all_gather | solution.py:24
  69.9 0.0 copy-start.3
  69.9 0.0 copy-start.4
  69.9 2.7 fusion.6
  72.7 0.0 copy-done.3
  72.7 0.0 copy-done.4
  72.7 3.9 %fusion.8 = f32[640,2560]{1,0:T(8,128)} fusion(bf16[512,2560]{1,0:T(8,128)(2,1)S(1)} %copy-done.3, s32[]{:T(128)S(6)} %select_n.31, bf16[512,640]{1,0:T(8,128)(2,1)S(1)} %copy-done.4, pred[256]{0:T(512)(128)(4,1)S(1)} %compare_and_fusion.2), kind=kOutput, calls=%fused_computation.18 | convolution fusion | flops 839024640 | bytes 8193536 | tf_op jit(solution)/shard_map/dot_general | solution.py:40
  76.6 3.9 %fusion.4 = f32[640,2560]{1,0:T(8,128)} fusion(bf16[512,2560]{1,0:T(8,128)(2,1)S(1)} %copy-done.3, s32[]{:T(128)S(6)} %select_n.35, bf16[512,640]{1,0:T(8,128)(2,1)S(1)} %copy-done.4, pred[256]{0:T(512)(128)(4,1)S(1)} %compare_and_fusion), kind=kOutput, calls=%fused_computation.14 | convolution fusion | flops 839024640 | bytes 8193536 | tf_op jit(solution)/shard_map/dot_general | solution.py:40
  80.5 17.2 %multiply_add_fusion = (f32[640,2560]{1,0:T(8,128)}, bf16[1,640,2560]{2,1,0:T(8,128)(2,1)}, bf16[1,640,2560]{2,1,0:T(8,128)(2,1)}, bf16[1,640,2560]{2,1,0:T(8,128)(2,1)}, bf16[1,640,2560]{2,1,0:T(8,128)(2,1)}) fusion(f32[640,2560]{1,0:T(8,128)} %fusion.4, f32[640,2560]{1,0:T(8,128)S(1)} %fusion.6, f32[640,2560]{1,0:T(8,128)} %fusion.8, ...), kind=kOutput, calls=%fused_computation.4 | convolution fusion | flops 857047040 | bytes 40961536 | tf_op jit(solution)/shard_map/dot_general | solution.py:40
  97.6 0.0 all-reduce.2.cloned.1.call-update
  97.6 2.8 %convolution_convert_fusion.2 = bf16[128,640]{1,0:T(8,128)(2,1)S(1)} fusion(bf16[128,2560]{1,0:T(8,128)(2,1)} %param.10, bf16[2560,640]{1,0:T(8,128)(2,1)} %param.12), kind=kOutput, calls=%fused_computation.22 | convolution fusion | flops 419512320 | bytes 4096000 | tf_op jit(solution)/shard_map/dot_general | solution.py:14
  100.5 17.4 %all_gather.6 = bf16[128,2560]{1,0:T(8,128)(2,1)} all-gather(bf16[128,640]{1,0:T(8,128)(2,1)S(1)} %convolution_convert_fusion.2), channel_id=1, replica_groups=mesh['dp'=8,'mp'=4] {'mp'}, dimensions={1}, use_global_device_ids=true | all-gather | bytes 819200 | tf_op jit(solution)/shard_map/all_gather | solution.py:25
  117.9 85.4 %all-reduce.2.cloned.1.call-done = f32[640,2560]{1,0:T(8,128)} async-done(((f32[640,2560]{1,0:T(8,128)}), f32[640,2560]{1,0:T(8,128)}) %all-reduce.2.cloned.1.call-update) | async-done | bytes 6553616 | tf_op jit(solution)/shard_map/psum | solution.py:48
  203.3 0.0 copy-start.1
  203.3 0.0 copy-start.2
  203.3 5.3 %multiply_reduce_fusion = f32[]{:T(128)} fusion(f32[640,2560]{1,0:T(8,128)} %all-reduce.2.cloned.1.call-done), kind=kLoop, calls=%fused_computation.6 | loop fusion | flops 3276799 | bytes 6553604 | tf_op jit(solution)/shard_map/reduce_sum | solution.py:49
  208.6 0.0 copy-done.1
  208.6 0.0 copy-done.2
  208.6 8.7 %pad_maximum_fusion = bf16[4,640,2560]{2,1,0:T(8,128)(2,1)} fusion(bf16[1,640,2560]{2,1,0:T(8,128)(2,1)} %get-tuple-element.9, bf16[1,640,2560]{2,1,0:T(8,128)(2,1)} %get-tuple-element.8, bf16[1,640,2560]{2,1,0:T(8,128)(2,1)S(1)} %copy-done.2, bf16[1,640,2560]{2,1,0:T(8,128)(2,1)S(1)} %copy-done.1), kind=kLoop, calls=%fused_computation | loop fusion | flops 19660800 | bytes 26214400 | tf_op jit(solution)/shard_map/stack | solution.py:45
  217.3 12.5 %psum.22 = f32[]{:T(128)} all-reduce(f32[]{:T(128)} %multiply_reduce_fusion), channel_id=1, replica_groups=mesh['dp'=8,'mp'=4] {'mp'}, use_global_device_ids=true, to_apply=%region_3.4 | all-reduce | flops 1 | bytes 8 | tf_op jit(solution)/shard_map/psum | solution.py:49
  230.4 6.7 %fusion.3 = bf16[640,2560,1]{1,0,2:T(8,128)(2,1)} fusion(f32[640,2560]{1,0:T(8,128)} %all-reduce.2.cloned.1.call-done, bf16[128,2560]{1,0:T(8,128)(2,1)} %all_gather.6, f32[]{:T(128)S(6)} %div.7, bf16[128,2560]{1,0:T(8,128)(2,1)} %param.11, bf16[2560,640]{1,0:T(8,128)(2,1)S(1)} %copy-done), kind=kOutput, calls=%fused_computation.7 | convolution fusion | flops 845496320 | bytes 14417924 | tf_op jit(solution)/shard_map/qti,qtj->qij/dot_general | solution.py:51
  237.1 23.7 %fusion.12 = f32[1,4]{1,0:T(1,128)S(1)} fusion(bf16[4,640,2560]{2,1,0:T(8,128)(2,1)} %pad_maximum_fusion, bf16[640,2560,1]{1,0,2:T(8,128)(2,1)} %fusion.3), kind=kOutput, calls=%fused_computation.24 | convolution fusion | flops 13107200 | bytes 16384016 | tf_op jit(solution)/shard_map/qik,sik->qs/dot_general | solution.py:55
  260.8 8.9 %psum.23 = f32[1,4]{1,0:T(1,128)} all-reduce(f32[1,4]{1,0:T(1,128)S(1)} %fusion.12), channel_id=1, replica_groups=mesh['dp'=8,'mp'=4] {'mp'}, use_global_device_ids=true, to_apply=%region_4.5 | all-reduce | flops 4 | bytes 32 | tf_op jit(solution)/shard_map/psum | solution.py:56
  (1 shorter events, 0.0 us)
Async XLA Ops:
  6.5 15.0 %copy-start = (bf16[2560,640]{1,0:T(8,128)(2,1)S(1)}, bf16[2560,640]{1,0:T(8,128)(2,1)}, u32[]{:S(2)}) copy-start(bf16[2560,640]{1,0:T(8,128)(2,1)} %param.13) | copy-start | bytes 9830404
  6.5 6.0 %copy-start.5 = (s32[4]{0:T(128)S(1)}, s32[4]{0:T(128)}, u32[]{:S(2)}) copy-start(s32[4]{0:T(128)} %param.9) | copy-start | bytes 52
  6.5 63.4 %all-gather.2.cloned.1.call-start = ((), (), s32[]{:S(2)}) async-start(), calls=%async_computation | async-start | bytes 3276800 | tf_op jit(solution)/shard_map/all_gather | solution.py:24
  12.5 190.8 %all-reduce.2.cloned.1.call-start = ((), (), s32[]{:S(2)}) async-start(), calls=%async_computation.1 | async-start | bytes 13107200 | tf_op jit(solution)/shard_map/psum | solution.py:48
  69.9 2.8 copy-start.3
  69.9 2.8 copy-start.4
  203.3 5.3 %copy-start.1 = (bf16[1,640,2560]{2,1,0:T(8,128)(2,1)S(1)}, bf16[1,640,2560]{2,1,0:T(8,128)(2,1)}, u32[]{:S(2)}) copy-start(bf16[1,640,2560]{2,1,0:T(8,128)(2,1)} %get-tuple-element.6) | copy-start | bytes 9830404
  203.3 5.3 %copy-start.2 = (bf16[1,640,2560]{2,1,0:T(8,128)(2,1)S(1)}, bf16[1,640,2560]{2,1,0:T(8,128)(2,1)}, u32[]{:S(2)}) copy-start(bf16[1,640,2560]{2,1,0:T(8,128)(2,1)} %get-tuple-element.7) | copy-start | bytes 9830404
Sparse Core Ops, SparseCore 0:
  12.6 57.2 all-gather.1
  97.8 105.4 all-reduce.1
where the time goes:
time: 277 us
  waiting for transfers between devices  129 us (47%)
  matrix products  71.8 us (26%)
  blocking collectives  38.7 us (14%)
  other arithmetic  19.2 us (7%)
  between operations  16.6 us (6%)
    psum x1, waiting for transfers between devices, shards(): curvature = lax.psum(curvature_local, 'dp') * inverse_count  85.4 us
    all_gather x1, waiting for transfers between devices, shards(): lax.all_gather(acts_block, 'mp', axis=1, tiled=True)  43.4 us
    dot_general x4, matrix products, shards(): lax.dot_general(grads_win, acts_win, (((0,), (0,)), ((), ())), preferred_...  27.7 us
    dot_general x1, matrix products, shards(): jnp.einsum('qik,sik->qs', precond, stored, preferred_element_type=jnp.flo...  23.7 us
    all_gather x1, blocking collectives, shards(): lax.all_gather(query_block, 'mp', axis=1, tiled=True)  17.4 us
    dot_general x3, matrix products, rotate(): jnp.dot(values, basis, preferred_element_type=jnp.float32)  13.7 us
    psum x1, blocking collectives, shards(): grand_total = lax.psum(jnp.sum(curvature), 'mp')  12.5 us
    psum x1, blocking collectives, shards(): return lax.psum(partial_value, 'mp')  8.86 us
  transfers between devices with their start and end apart: 2, of which 2 were waited for; matrix products, arithmetic and copies ran while one was open for 5% of the time, Pallas kernels for 0%

commit v1 on v0

v1 whole, which is shorter than its diff:
```python
import functools

import jax
import jax.numpy as jnp
from jax import lax
from jax.experimental import pallas as pl
from jax.experimental.pallas import tpu as pltpu
from jax.sharding import PartitionSpec as P

damping_ratio = 0.1
MESH = pl.DeviceIdType.MESH
VMEM = pl.BlockSpec(memory_space=pltpu.VMEM)
GRANT = 56 * 1024 * 1024


def rotate(values, basis):
    return jnp.dot(values, basis, preferred_element_type=jnp.float32).astype(jnp.bfloat16)


def remote(src, dst, send, recv, d, m):
    return pltpu.make_async_remote_copy(
        src_ref=src, dst_ref=dst, send_sem=send, recv_sem=recv, device_id=(d, m), device_id_type=MESH
    )


def spread_kernel(mp, a, g, q, s, a2, gs, q2, ss, a_send, a_recv, q_send, q_recv, o_send, o_recv):
    d, m = lax.axis_index("dp"), lax.axis_index("mp")
    rows, cols = a.shape
    half = mp // 2
    core = lax.rem(d, 2)
    base = d - core
    sibling = base + 1 - core
    owner = m // half
    place = lax.rem(m, half)

    def a_slot(c, j):
        return a2.at[pl.ds(pl.multiple_of(c * rows, rows), rows), pl.ds(pl.multiple_of(j * cols, cols), cols)]

    def q_slot(j):
        return q2.at[:, pl.ds(pl.multiple_of(j * cols, cols), cols)]

    def a_copy(k):
        return remote(a, a_slot(core, place), a_send.at[k], a_recv.at[core, place], base + owner, lax.rem(m + k, mp))

    def q_copy(k):
        return remote(q, q_slot(place), q_send.at[k], q_recv.at[place], d, lax.rem(m + k, mp))

    g_copy = remote(g, gs, o_send.at[0], o_recv.at[0], sibling, m)
    s_copy = remote(s, ss, o_send.at[1], o_recv.at[1], sibling, m)
    order = [mp // 2] + [k for k in range(1, mp) if k != mp // 2]
    for k in order:
        a_copy(k).start()
    g_copy.start()
    s_copy.start()

    @pl.when(owner == core)
    def _():
        pltpu.make_async_copy(a, a_slot(core, place), a_recv.at[core, place]).start()
        pltpu.make_async_copy(q, q_slot(place), q_recv.at[place]).start()
        for k in order:
            q_copy(k).start()

    @pl.when(owner != core)
    def _():
        a_copy(0).start()

    for c in range(2):
        for j in range(half):
            pltpu.make_async_copy(a, a_slot(c, j), a_recv.at[c, j]).wait()
    for j in range(half):
        pltpu.make_async_copy(q, q_slot(j), q_recv.at[j]).wait()
    for k in range(1, mp):
        a_copy(k).wait_send()

    @pl.when(owner == core)
    def _():
        for k in range(1, mp):
            q_copy(k).wait_send()

    @pl.when(owner != core)
    def _():
        a_copy(0).wait_send()

    g_copy.wait()
    s_copy.wait()


def spread(mp, a, g, q, s):
    rows, cols = a.shape
    half = mp // 2
    dma = pltpu.SemaphoreType.DMA
    return pl.pallas_call(
        functools.partial(spread_kernel, mp),
        out_shape=[
            jax.ShapeDtypeStruct((2 * rows, half * cols), a.dtype),
            jax.ShapeDtypeStruct(g.shape, g.dtype),
            jax.ShapeDtypeStruct((q.shape[0], half * cols), q.dtype),
            jax.ShapeDtypeStruct(s.shape, s.dtype),
        ],
        in_specs=[VMEM] * 4,
        out_specs=[VMEM] * 4,
        scratch_shapes=[dma((mp,)), dma((2, half)), dma((mp,)), dma((half,)), dma((2,)), dma((2,))],
        compiler_params=pltpu.CompilerParams(has_side_effects=True, vmem_limit_bytes=GRANT),
        name="spread",
    )(a, g, q, s)


def square_kernel(slots, g0, g1, a2, c, sums):
    rows = a2.shape[0] // 2
    width = c.shape[0]
    total = None
    for g, at in ((g0, 0), (g1, rows)):
        for slot in range(slots):
            p = jnp.dot(
                g[slot * width:(slot + 1) * width, :], a2[at:at + rows, :], preferred_element_type=jnp.float32
            )
            total = p * p if total is None else total + p * p
    c[...] = total.astype(c.dtype)
    sums[...] = jnp.sum(total, axis=0, keepdims=True)


def squares(slots, g0, g1, a2, tile):
    rows2, cols = a2.shape
    width = g0.shape[0] // slots
    whole = lambda j: (0, 0)
    part = lambda j: (0, j)
    return pl.pallas_call(
        functools.partial(square_kernel, slots),
        grid=(cols // tile,),
        out_shape=[
            jax.ShapeDtypeStruct((width, cols), jnp.bfloat16),
            jax.ShapeDtypeStruct((1, cols), jnp.float32),
        ],
        in_specs=[
            pl.BlockSpec(g0.shape, whole),
            pl.BlockSpec(g1.shape, whole),
            pl.BlockSpec((rows2, tile), part),
        ],
        out_specs=[pl.BlockSpec((width, tile), part), pl.BlockSpec((1, tile), part)],
        compiler_params=pltpu.CompilerParams(vmem_limit_bytes=GRANT),
        name="squares",
    )(g0, g1, a2)


def piece(ref, across, shape, p):
    high, wide = shape
    return ref.at[
        pl.ds(pl.multiple_of((p // across) * high, high), high),
        pl.ds(pl.multiple_of(lax.rem(p, across) * wide, wide), wide),
    ]


def scatter_kernel(n, mp, across, shape, c, t, r, tt, c_send, c_recv, t_send, t_recv, u_send, u_recv):
    d, m = lax.axis_index("dp"), lax.axis_index("mp")
    core = lax.rem(d, 2)
    chip = d // 2
    base = d - core
    near = 2 * mp
    me = core * mp + m

    def c_copy(k):
        p = lax.rem(chip + k, n)
        return remote(piece(c, across, shape, p), r.at[chip], c_send.at[k], c_recv.at[chip], 2 * p + core, m)

    def t_copy(k):
        o = lax.rem(me + k, near)
        return remote(t, tt.at[chip, me], t_send.at[k], t_recv.at[me], base + o // mp, lax.rem(o, mp))

    def u_copy(k):
        p = lax.rem(chip + k, n)
        return remote(tt.at[chip], tt.at[chip], u_send.at[k], u_recv.at[chip], 2 * p + core, m)

    for k in range(1, near):
        t_copy(k).start()
    pltpu.make_async_copy(t, tt.at[chip, me], t_recv.at[me]).start()
    for k in range(1, n):
        c_copy(k).start()
    pltpu.make_async_copy(piece(c, across, shape, chip), r.at[chip], c_recv.at[chip]).start()
    for o in range(near):
        pltpu.make_async_copy(t, tt.at[chip, o], t_recv.at[o]).wait()
    for k in range(1, n):
        u_copy(k).start()
    for k in range(1, near):
        t_copy(k).wait_send()
    for k in range(1, n):
        p = lax.rem(chip + k, n)
        pltpu.make_async_copy(tt.at[chip], tt.at[p], u_recv.at[p]).wait()
        u_copy(k).wait_send()
        c_copy(k).wait_send()
    for p in range(n):
        pltpu.make_async_copy(piece(c, across, shape, chip), r.at[p], c_recv.at[p]).wait()


def scatter(n, mp, across, shape, c, t):
    dma = pltpu.SemaphoreType.DMA
    return pl.pallas_call(
        functools.partial(scatter_kernel, n, mp, across, shape),
        out_shape=[
            jax.ShapeDtypeStruct((n,) + shape, c.dtype),
            jax.ShapeDtypeStruct((n, 2 * mp) + t.shape, t.dtype),
        ],
        in_specs=[VMEM] * 2,
        out_specs=[VMEM] * 2,
        scratch_shapes=[dma((n,)), dma((n,)), dma((2 * mp,)), dma((2 * mp,)), dma((n,)), dma((n,))],
        compiler_params=pltpu.CompilerParams(has_side_effects=True, vmem_limit_bytes=GRANT),
        name="scatter",
    )(c, t)


def collect_kernel(n, across, shape, x, out, send, recv):
    d, m = lax.axis_index("dp"), lax.axis_index("mp")
    core = lax.rem(d, 2)
    chip = d // 2
    here = piece(out, across, shape, chip)

    def copy(k):
        return remote(x, here, send.at[k], recv.at[chip], 2 * lax.rem(chip + k, n) + core, m)

    for k in range(1, n):
        copy(k).start()
    pltpu.make_async_copy(x, here, recv.at[chip]).start()
    for p in range(n):
        pltpu.make_async_copy(x, piece(out, across, shape, p), recv.at[p]).wait()
    for k in range(1, n):
        copy(k).wait_send()


def collect(n, across, shape, full, x):
    dma = pltpu.SemaphoreType.DMA
    return pl.pallas_call(
        functools.partial(collect_kernel, n, across, shape),
        out_shape=jax.ShapeDtypeStruct(full, x.dtype),
        in_specs=[VMEM],
        out_specs=VMEM,
        scratch_shapes=[dma((n,)), dma((n,))],
        compiler_params=pltpu.CompilerParams(has_side_effects=True, vmem_limit_bytes=GRANT),
        name="collect",
    )(x)


def score_kernel(g0, g1, a2, p, out):
    rows = g0.shape[0]

    @pl.when(pl.program_id(0) == 0)
    def _():
        out[...] = jnp.zeros_like(out)

    for g, at in ((g0, 0), (g1, rows)):
        y = jnp.dot(g[...], p[...], preferred_element_type=jnp.float32)
        z = y * a2[at:at + rows, :].astype(jnp.float32)
        total = z[:, :128]
        for lane in range(128, z.shape[1], 128):
            total = total + z[:, lane:lane + 128]
        out[at:at + rows, :] += total


def token_scores(g0, g1, a2, p, tile):
    rows2, cols = a2.shape
    whole = lambda j: (0, 0)
    part = lambda j: (0, j)
    return pl.pallas_call(
        score_kernel,
        grid=(cols // tile,),
        out_shape=jax.ShapeDtypeStruct((rows2, 128), jnp.float32),
        in_specs=[
            pl.BlockSpec(g0.shape, whole),
            pl.BlockSpec(g1.shape, whole),
            pl.BlockSpec((rows2, tile), part),
            pl.BlockSpec((p.shape[0], tile), part),
        ],
        out_specs=pl.BlockSpec((rows2, 128), whole),
        compiler_params=pltpu.CompilerParams(vmem_limit_bytes=GRANT),
        name="token_scores",
    )(g0, g1, a2, p)


def finish_kernel(mp, t, out, send, recv):
    d, m = lax.axis_index("dp"), lax.axis_index("mp")
    core = lax.rem(d, 2)
    base = d - core
    near = 2 * mp
    me = core * mp + m

    def copy(k):
        o = lax.rem(me + k, near)
        return remote(t, out.at[me], send.at[k], recv.at[me], base + o // mp, lax.rem(o, mp))

    for k in range(1, near):
        copy(k).start()
    pltpu.make_async_copy(t, out.at[me], recv.at[me]).start()
    for o in range(near):
        pltpu.make_async_copy(t, out.at[o], recv.at[o]).wait()
    for k in range(1, near):
        copy(k).wait_send()


def share(mp, t):
    dma = pltpu.SemaphoreType.DMA
    return pl.pallas_call(
        functools.partial(finish_kernel, mp),
        out_shape=jax.ShapeDtypeStruct((2 * mp,) + t.shape, t.dtype),
        in_specs=[VMEM],
        out_specs=VMEM,
        scratch_shapes=[dma((2 * mp,)), dma((2 * mp,))],
        compiler_params=pltpu.CompilerParams(has_side_effects=True),
        name="share",
    )(t)


def shards(dp, mp, train_acts, train_grads, lengths, query_acts, query_grads, basis_in, basis_out):
    rows = train_acts.shape[0]
    width = basis_in.shape[1]
    slots = lengths.shape[0]
    n = dp // 2
    cols = (mp // 2) * basis_in.shape[1]
    down = max(
        k for k in range(1, n + 1) if n % k == 0 and width % (8 * k) == 0 and cols % (128 * (n // k)) == 0
    )
    across = n // down
    shape = (width // down, cols // across)
    tile = 256
    core = lax.axis_index("dp") % 2
    chip = lax.axis_index("dp") // 2

    finish = jnp.cumsum(lengths)
    slot_of = jnp.sum(jnp.arange(rows, dtype=jnp.int32)[None, :] >= finish[:, None], axis=0)
    slot_rows = jnp.broadcast_to(slot_of.astype(jnp.float32)[None, :], (8, rows))
    acts_block = rotate(train_acts, basis_in)
    grads_own = rotate(train_grads, basis_out)
    query_block = rotate(query_acts, basis_in)
    query_grot = rotate(query_grads, basis_out)
    acts2, grads_sib, query2, slot_sib = spread(mp, acts_block, grads_own, query_block, slot_rows)

    own_first = core == 0
    grads0 = jnp.where(own_first, grads_own, grads_sib)
    grads1 = jnp.where(own_first, grads_sib, grads_own)
    slot0 = jnp.where(own_first, slot_rows[0], slot_sib[0])
    slot1 = jnp.where(own_first, slot_sib[0], slot_rows[0])
    names = jnp.arange(slots, dtype=jnp.float32)
    mask0 = names[:, None] == slot0[None, :]
    mask1 = names[:, None] == slot1[None, :]

    def masked(grads, mask):
        turned = grads.T
        return jnp.where(mask[:, None, :], turned[None], jnp.zeros_like(turned)[None]).reshape(slots * width, rows)

    squared, sums = squares(slots, masked(grads0, mask0), masked(grads1, mask1), acts2, tile)
    total = jnp.broadcast_to(jnp.sum(sums), (8, 128))
    pieces, totals = scatter(n, mp, across, shape, squared, total)

    sequences = slots * dp
    curvature = jnp.sum(pieces.astype(jnp.float32), axis=0) / sequences
    entries = width * mp * width * mp
    damping = damping_ratio * (jnp.sum(totals[:, :, 0, 0]) / sequences / entries)
    row_at = (chip // across) * shape[0]
    col_at = (chip % across) * shape[1]
    left = lax.dynamic_slice_in_dim(query_grot, row_at, shape[0], 1)
    right = lax.dynamic_slice_in_dim(query2, col_at, shape[1], 1)
    local_grad = lax.dot_general(left, right, (((0,), (0,)), ((), ())), preferred_element_type=jnp.float32)
    precond = (local_grad / (curvature + damping)).astype(jnp.bfloat16)
    precond_full = collect(n, across, shape, (width, cols), precond)

    by_token = jnp.sum(token_scores(grads0, grads1, acts2, precond_full, tile), axis=1)
    partial0 = jnp.sum(jnp.where(mask0, by_token[None, :rows], 0.0), axis=1)
    partial1 = jnp.sum(jnp.where(mask1, by_token[None, rows:], 0.0), axis=1)
    packed = jnp.zeros((8, 128), jnp.float32).at[0, :slots].set(partial0).at[1, :slots].set(partial1)
    summed = jnp.sum(share(mp, packed), axis=0)
    return jnp.where(own_first, summed[0:1, :slots], summed[1:2, :slots])


def solution(mesh):
    return jax.shard_map(
        functools.partial(shards, mesh.shape["dp"], mesh.shape["mp"]),
        mesh=mesh,
        in_specs=(P("dp", None), P("dp", None), P("dp"), P(), P(), P(None, "mp"), P(None, "mp")),
        out_specs=P(None, "dp"),
        check_vma=False,
    )
```

time: 277 us -> 203 us (0.73)
  Pallas kernels: 0 us -> 161 us
  waiting for transfers between devices: 129 us -> 0 us
  matrix products: 71.8 us -> 14.5 us
  blocking collectives: 38.7 us -> 0 us
  between operations: 16.6 us -> 0.76 us
  local copies, waits for them, and re-layouts: 1.31 us -> 9.67 us
    pallas_call x0 -> x6, Pallas kernels: none -> 161 us  [the longest x1 58.7 us: spread(): pl.pallas_call(functools.partial(spread_kernel, mp), out_shape=[jax.Shape...]
    psum x1 -> x0, waiting for transfers between devices: 85.4 us -> none  [shards(): curvature = lax.psum(curvature_local, 'dp') * inverse_count]
    dot_general x6 -> x1, matrix products: 58.1 us -> 2.39 us  [shards(): lax.dot_general(left, right, (((0,), (0,)), ((), ())), preferred_element_...]
    all_gather x1 -> x0, waiting for transfers between devices: 43.4 us -> none  [shards(): lax.all_gather(acts_block, 'mp', axis=1, tiled=True)]
    psum x2 -> x0, blocking collectives: 21.3 us -> none  [the longest x1 12.5 us: shards(): grand_total = lax.psum(jnp.sum(curvature), 'mp')]
    all_gather x1 -> x0, blocking collectives: 17.4 us -> none  [shards(): lax.all_gather(query_block, 'mp', axis=1, tiled=True)]
    another operation x2 -> x1, other arithmetic: 8.92 us -> 0.18 us  [the longest x1 8.74 us: shards(): stored = jnp.stack(stored_list)]
    select_n x0 -> x5, other arithmetic: none -> 8.59 us  [the longest x2 5.62 us: masked(): jnp.where(mask[:, None, :], turned[None], jnp.zeros_like(turned)[None])]
  transfers between devices with their start and end apart: 2 -> 0, of which waited for: 2 -> 0; matrix products, arithmetic and copies ran while one was open for 5% -> 0% of each run, Pallas kernels for 0% -> 0%
where the time goes in v1:
time: 203 us; the launch traced here: 202 us
  Pallas kernels  161 us (79%)
  other arithmetic  16.5 us (8%)
  matrix products  14.5 us (7%)
  local copies, waits for them, and re-layouts  9.67 us (5%)
    pallas_call x1, Pallas kernels, spread(): pl.pallas_call(functools.partial(spread_kernel, mp), out_shape=[jax.Shape...  58.7 us
    pallas_call x1, Pallas kernels, scatter(): pl.pallas_call(functools.partial(scatter_kernel, n, mp, across, shape), o...  46.6 us
    pallas_call x1, Pallas kernels, collect(): pl.pallas_call(functools.partial(collect_kernel, n, across, shape), out_s...  26.6 us
    dot_general x4, matrix products, rotate(): jnp.dot(values, basis, preferred_element_type=jnp.float32)  12.1 us
    pallas_call x1, Pallas kernels, share(): pl.pallas_call(functools.partial(finish_kernel, mp), out_shape=jax.ShapeD...  11.3 us
    pallas_call x1, Pallas kernels, squares(): pl.pallas_call(functools.partial(square_kernel, slots), grid=(cols // til...  11.3 us
    pallas_call x1, Pallas kernels, token_scores(): pl.pallas_call(score_kernel, grid=(cols // tile,), out_shape=jax.ShapeDty...  6.46 us
    select_n x2, other arithmetic, masked(): jnp.where(mask[:, None, :], turned[None], jnp.zeros_like(turned)[None])  5.62 us

profile of v1, /device:TPU:0, one launch (start us, length us, event | category | flops | bytes accessed | tf_op | source)
XLA Modules:
  0.0 202.3 jit_solution(6910340082844900078)
XLA Ops:
  0.0 0.0 copy-start
  0.0 1.9 copy-done
  1.9 0.0 copy-start.1
  1.9 0.0 copy-start.4
  1.9 4.9 %convolution_convert_fusion.1.a = bf16[512,640]{1,0:T(8,128)(2,1)} fusion(bf16[512,2560]{1,0:T(8,128)(2,1)} %param.11, bf16[2560,640]{1,0:T(8,128)(2,1)S(1)} %copy-done), kind=kOutput, calls=%fused_computation.6 | convolution fusion | flops 1678049280 | bytes 6553600 | tf_op jit(solution)/shard_map/dot_general | solution.py:17
  6.9 0.0 copy-done.1
  6.9 0.0 copy-done.4
  6.9 0.0 copy-start.2
  6.9 3.0 %convolution_convert_fusion.g = bf16[512,640]{1,0:T(8,128)(2,1)} fusion(bf16[512,2560]{1,0:T(8,128)(2,1)S(1)} %copy-done.4, bf16[2560,640]{1,0:T(8,128)(2,1)S(1)} %copy-done.1), kind=kOutput, calls=%fused_computation.5 | convolution fusion | flops 1678049280 | bytes 6553600 | tf_op jit(solution)/shard_map/dot_general | solution.py:17
  9.9 0.0 copy-done.2
  9.9 0.0 copy-start.5
  9.9 1.3 convolution_convert_fusion.2.q
  11.3 0.0 copy-done.5
  11.3 0.2 reduce-window.8
  11.4 0.1 convert_reduce_fusion.1
  11.5 0.6 broadcast_in_dim.77.s
  12.1 58.7 %spread.1 = (bf16[1024,1280]{1,0:T(8,128)(2,1)}, bf16[512,640]{1,0:T(8,128)(2,1)}, bf16[128,1280]{1,0:T(8,128)(2,1)}, f32[8,512]{1,0:T(8,128)}) custom-call(bf16[512,640]{1,0:T(8,128)(2,1)} %convolution_convert_fusion.1.a, bf16[512,640]{1,0:T(8,128)(2,1)} %convolution_convert_fusion.g, bf16[128,640]{1,0:T(8,128)(2,1)} %convolution_convert_fusion.2.q, ...), custom_call_target="tpu_custom_call" | custom-call | tf_op jit(solution)/shard_map/spread/pallas_call | solution.py:92
  70.8 2.5 %broadcast_select_fusion.2 = (bf16[512,640]{1,0:T(8,128)(2,1)}, bf16[512,640]{1,0:T(8,128)(2,1)}) fusion(bf16[512,640]{1,0:T(8,128)(2,1)} %get-tuple-element.38, bf16[512,640]{1,0:T(8,128)(2,1)} %convolution_convert_fusion.g, pred[]{:T(512)S(6)} %eq.40), kind=kLoop, calls=%fused_computation.8 | loop fusion | flops 655360 | bytes 2621441 | tf_op jit(solution)/shard_map/jit(_where)/select_n | solution.py:336
  73.3 0.7 slice.56
  74.0 2.2 %copy.10 = bf16[640,512]{1,0:T(8,128)(2,1)} copy(bf16[640,512]{0,1:T(8,128)(2,1)} %bitcast.21) | data formatting | bytes 1310720 | tf_op jit(solution)/shard_map/transpose | solution.py:344
  76.2 2.8 %broadcast_select_fusion.1 = bf16[4,640,512]{2,1,0:T(8,128)(2,1)} fusion(pred[4,512]{1,0:T(4,128)(4,1)S(1)} %iota_compare_fusion.2, bf16[640,512]{1,0:T(8,128)(2,1)} %copy.10), kind=kLoop, calls=%fused_computation.2 | loop fusion | flops 1310720 | bytes 3278848 | tf_op jit(solution)/shard_map/jit(_where)/select_n | solution.py:345
  79.0 2.2 %copy.11 = bf16[640,512]{1,0:T(8,128)(2,1)} copy(bf16[640,512]{0,1:T(8,128)(2,1)} %bitcast.20) | data formatting | bytes 1310720 | tf_op jit(solution)/shard_map/transpose | solution.py:344
  81.2 2.8 %broadcast_select_fusion = bf16[4,640,512]{2,1,0:T(8,128)(2,1)} fusion(pred[4,512]{1,0:T(4,128)(4,1)S(1)} %iota_compare_fusion, bf16[640,512]{1,0:T(8,128)(2,1)} %copy.11), kind=kLoop, calls=%fused_computation.1 | loop fusion | flops 1310720 | bytes 3278848 | tf_op jit(solution)/shard_map/jit(_where)/select_n | solution.py:345
  84.0 11.3 %squares.1 = (bf16[640,1280]{1,0:T(8,128)(2,1)}, f32[1,1280]{1,0:T(1,128)}) custom-call(bf16[2560,512]{1,0:T(8,128)(2,1)} %bitcast.18, bf16[2560,512]{1,0:T(8,128)(2,1)} %bitcast.19, bf16[1024,1280]{1,0:T(8,128)(2,1)} %get-tuple-element.39.a2), custom_call_target="tpu_custom_call" | custom-call | tf_op jit(solution)/shard_map/squares/pallas_call | solution.py:127
  95.3 1.3 reduce_sum.73
  96.6 1.2 broadcast_in_dim.83.t
  97.8 46.6 %scatter.13 = (bf16[4,160,1280]{2,1,0:T(8,128)(2,1)}, f32[4,8,8,128]{3,2,1,0:T(8,128)}) custom-call(bf16[640,1280]{1,0:T(8,128)(2,1)} %get-tuple-element.41.c, f32[8,128]{1,0:T(8,128)} %broadcast_in_dim.83.t), custom_call_target="tpu_custom_call" | custom-call | tf_op jit(solution)/shard_map/scatter/pallas_call | solution.py:196
  144.4 2.6 %convert_reduce_fusion = f32[160,1280]{1,0:T(8,128)} fusion(bf16[4,160,1280]{2,1,0:T(8,128)(2,1)} %get-tuple-element.43), kind=kLoop, calls=%fused_computation | loop fusion | flops 1433600 | bytes 2457600 | tf_op jit(solution)/shard_map/reduce_sum | solution.py:352
  147.1 1.5 slice_reduce_fusion
  149.3 2.8 %fusion.3 = bf16[128,640]{1,0:T(8,128)(2,1)S(1)} fusion(bf16[128,2560]{1,0:T(8,128)(2,1)} %param.15, bf16[2560,640]{1,0:T(8,128)(2,1)} %param.17), kind=kOutput, calls=%fused_computation.23 | convolution fusion | flops 419430400 | bytes 4096000 | tf_op jit(solution)/shard_map/dot_general | solution.py:17
  152.1 2.4 %fusion.x = bf16[160,1280]{1,0:T(8,128)(2,1)} fusion(bf16[128,1280]{1,0:T(8,128)(2,1)} %get-tuple-element.40, f32[160,1280]{1,0:T(8,128)} %convert_reduce_fusion, f32[]{:T(128)S(6)} %mul_shard_map.3, bf16[128,640]{1,0:T(8,128)(2,1)S(1)} %fusion.3, s32[]{:T(128)S(6)} %select_n.80), kind=kOutput, calls=%fused_computation.4 | convolution fusion | flops 53248000 | bytes 1622024 | tf_op jit(solution)/shard_map/dot_general | solution.py:359
  154.5 26.6 %collect.1.p = bf16[640,1280]{1,0:T(8,128)(2,1)} custom-call(bf16[160,1280]{1,0:T(8,128)(2,1)} %fusion.x), custom_call_target="tpu_custom_call" | custom-call | tf_op jit(solution)/shard_map/collect/pallas_call | solution.py:230
  181.1 6.5 %token_scores.1 = f32[1024,128]{1,0:T(8,128)} custom-call(bf16[512,640]{1,0:T(8,128)(2,1)} %get-tuple-element.46.g0, bf16[512,640]{1,0:T(8,128)(2,1)} %get-tuple-element.45.g1, bf16[1024,1280]{1,0:T(8,128)(2,1)} %get-tuple-element.39.a2, bf16[640,1280]{1,0:T(8,128)(2,1)} %collect.1.p), custom_call_target="tpu_custom_call" | custom-call | tf_op jit(solution)/shard_map/token_scores/pallas_call | solution.py:261
  187.5 1.2 reduce_sum.76
  188.8 0.2 select_reduce_fusion
  189.0 0.2 scatter.12.t
  189.2 0.0 copy-start.3
  189.2 0.6 copy-done.3
  189.7 11.3 %share.1 = f32[8,8,128]{2,1,0:T(8,128)} custom-call(f32[8,128]{1,0:T(8,128)} %copy-done.3), custom_call_target="tpu_custom_call" | custom-call | tf_op jit(solution)/shard_map/share/pallas_call | solution.py:299
  201.0 0.8 reduce_sum.79
  201.8 0.5 broadcast_select_fusion.6
  (6 shorter events, 0.1 us)
Async XLA Ops:
  0.0 1.9 copy-start
  1.9 4.9 %copy-start.1 = (bf16[2560,640]{1,0:T(8,128)(2,1)S(1)}, bf16[2560,640]{1,0:T(8,128)(2,1)}, u32[]{:S(2)}) copy-start(bf16[2560,640]{1,0:T(8,128)(2,1)} %param.17) | copy-start | bytes 9830404
  1.9 4.9 %copy-start.4 = (bf16[512,2560]{1,0:T(8,128)(2,1)S(1)}, bf16[512,2560]{1,0:T(8,128)(2,1)}, u32[]{:S(2)}) copy-start(bf16[512,2560]{1,0:T(8,128)(2,1)} %param.12) | copy-start | bytes 7864324
  6.9 3.0 %copy-start.2 = (bf16[128,2560]{1,0:T(8,128)(2,1)S(1)}, bf16[128,2560]{1,0:T(8,128)(2,1)}, u32[]{:S(2)}) copy-start(bf16[128,2560]{1,0:T(8,128)(2,1)} %param.14) | copy-start | bytes 1966084
  9.9 1.4 copy-start.5
  189.2 0.6 copy-start.3

commit v2 on v1

--- a/solution.py
+++ b/solution.py
@@ -23,7 +23,7 @@
     )
 
 
-def spread_kernel(mp, a, g, q, s, a2, gs, q2, ss, a_send, a_recv, q_send, q_recv, o_send, o_recv):
+def spread_kernel(mp, slots, a, g, gt, q, s, a2, g2, q2, s2, sq, sums, gt2, acc, a_send, a_recv, q_send, q_recv, o_send, o_recv):
     d, m = lax.axis_index("dp"), lax.axis_index("mp")
     rows, cols = a.shape
     half = mp // 2
@@ -45,13 +45,13 @@
     def q_copy(k):
         return remote(q, q_slot(place), q_send.at[k], q_recv.at[place], d, lax.rem(m + k, mp))
 
-    g_copy = remote(g, gs, o_send.at[0], o_recv.at[0], sibling, m)
-    s_copy = remote(s, ss, o_send.at[1], o_recv.at[1], sibling, m)
+    pairs = ((gt, gt2), (s, s2), (g, g2))
     order = [mp // 2] + [k for k in range(1, mp) if k != mp // 2]
     for k in order:
         a_copy(k).start()
-    g_copy.start()
-    s_copy.start()
+    for i, (src, dst) in enumerate(pairs):
+        remote(src, dst.at[core], o_send.at[i], o_recv.at[i, core], sibling, m).start()
+        pltpu.make_async_copy(src, dst.at[core], o_recv.at[i, core]).start()
 
     @pl.when(owner == core)
     def _():
@@ -64,9 +64,32 @@
     def _():
         a_copy(0).start()
 
-    for c in range(2):
-        for j in range(half):
+    for i, (src, dst) in enumerate(pairs):
+        for c in range(2):
+            pltpu.make_async_copy(src, dst.at[c], o_recv.at[i, c]).wait()
+
+    run = jnp.zeros((1, cols), jnp.float32)
+    for j in range(half):
+        acc[...] = jnp.zeros_like(acc)
+        for c in range(2):
             pltpu.make_async_copy(a, a_slot(c, j), a_recv.at[c, j]).wait()
+
+            def one(slot, carry):
+                mask = jnp.where(s2[c, 0:1, :] == slot.astype(jnp.float32), 1.0, 0.0).astype(gt2.dtype)
+                p = jnp.dot(
+                    gt2[c] * mask,
+                    a2[c * rows:(c + 1) * rows, j * cols:(j + 1) * cols],
+                    preferred_element_type=jnp.float32,
+                )
+                acc[...] += p * p
+                return carry
+
+            lax.fori_loop(0, slots, one, 0)
+        total = acc[...]
+        sq[:, j * cols:(j + 1) * cols] = total.astype(sq.dtype)
+        run = run + jnp.sum(total, axis=0, keepdims=True)
+    sums[...] = jnp.broadcast_to(jnp.sum(run, axis=1, keepdims=True), sums.shape)
+
     for j in range(half):
         pltpu.make_async_copy(q, q_slot(j), q_recv.at[j]).wait()
     for k in range(1, mp):
@@ -81,65 +104,34 @@
     def _():
         a_copy(0).wait_send()
 
-    g_copy.wait()
-    s_copy.wait()
-
-
-def spread(mp, a, g, q, s):
+    for i, (src, dst) in enumerate(pairs):
+        remote(src, dst.at[core], o_send.at[i], o_recv.at[i, core], sibling, m).wait_send()
+
+
+def spread(mp, slots, a, g, gt, q, s):
     rows, cols = a.shape
     half = mp // 2
     dma = pltpu.SemaphoreType.DMA
     return pl.pallas_call(
-        functools.partial(spread_kernel, mp),
+        functools.partial(spread_kernel, mp, slots),
         out_shape=[
             jax.ShapeDtypeStruct((2 * rows, half * cols), a.dtype),
-            jax.ShapeDtypeStruct(g.shape, g.dtype),
+            jax.ShapeDtypeStruct((2,) + g.shape, g.dtype),
             jax.ShapeDtypeStruct((q.shape[0], half * cols), q.dtype),
-            jax.ShapeDtypeStruct(s.shape, s.dtype),
+            jax.ShapeDtypeStruct((2,) + s.shape, s.dtype),
+            jax.ShapeDtypeStruct((g.shape[1], half * cols), jnp.bfloat16),
+            jax.ShapeDtypeStruct((8, 128), jnp.float32),
         ],
-        in_specs=[VMEM] * 4,
-        out_specs=[VMEM] * 4,
-        scratch_shapes=[dma((mp,)), dma((2, half)), dma((mp,)), dma((half,)), dma((2,)), dma((2,))],
+        in_specs=[VMEM] * 5,
+        out_specs=[VMEM] * 6,
+        scratch_shapes=[
+            pltpu.VMEM((2,) + gt.shape, gt.dtype),
+            pltpu.VMEM((g.shape[1], cols), jnp.float32),
+            dma((mp,)), dma((2, half)), dma((mp,)), dma((half,)), dma((3,)), dma((3, 2)),
+        ],
         compiler_params=pltpu.CompilerParams(has_side_effects=True, vmem_limit_bytes=GRANT),
         name="spread",
-    )(a, g, q, s)
-
-
-def square_kernel(slots, g0, g1, a2, c, sums):
-    rows = a2.shape[0] // 2
-    width = c.shape[0]
-    total = None
-    for g, at in ((g0, 0), (g1, rows)):
-        for slot in range(slots):
-            p = jnp.dot(
-                g[slot * width:(slot + 1) * width, :], a2[at:at + rows, :], preferred_element_type=jnp.float32
-            )
-            total = p * p if total is None else total + p * p
-    c[...] = total.astype(c.dtype)
-    sums[...] = jnp.sum(total, axis=0, keepdims=True)
-
-
-def squares(slots, g0, g1, a2, tile):
-    rows2, cols = a2.shape
-    width = g0.shape[0] // slots
-    whole = lambda j: (0, 0)
-    part = lambda j: (0, j)
-    return pl.pallas_call(
-        functools.partial(square_kernel, slots),
-        grid=(cols // tile,),
-        out_shape=[
-            jax.ShapeDtypeStruct((width, cols), jnp.bfloat16),
-            jax.ShapeDtypeStruct((1, cols), jnp.float32),
-        ],
-        in_specs=[
-            pl.BlockSpec(g0.shape, whole),
-            pl.BlockSpec(g1.shape, whole),
-            pl.BlockSpec((rows2, tile), part),
-        ],
-        out_specs=[pl.BlockSpec((width, tile), part), pl.BlockSpec((1, tile), part)],
-        compiler_params=pltpu.CompilerParams(vmem_limit_bytes=GRANT),
-        name="squares",
-    )(g0, g1, a2)
+    )(a, g, gt, q, s)
 
 
 def piece(ref, across, shape, p):
@@ -238,15 +230,15 @@
     )(x)
 
 
-def score_kernel(g0, g1, a2, p, out):
-    rows = g0.shape[0]
+def score_kernel(g2, a2, p, out):
+    rows = g2.shape[1]
 
     @pl.when(pl.program_id(0) == 0)
     def _():
         out[...] = jnp.zeros_like(out)
 
-    for g, at in ((g0, 0), (g1, rows)):
-        y = jnp.dot(g[...], p[...], preferred_element_type=jnp.float32)
+    for c, at in ((0, 0), (1, rows)):
+        y = jnp.dot(g2[c], p[...], preferred_element_type=jnp.float32)
         z = y * a2[at:at + rows, :].astype(jnp.float32)
         total = z[:, :128]
         for lane in range(128, z.shape[1], 128):
@@ -254,7 +246,7 @@
         out[at:at + rows, :] += total
 
 
-def token_scores(g0, g1, a2, p, tile):
+def token_scores(g2, a2, p, tile):
     rows2, cols = a2.shape
     whole = lambda j: (0, 0)
     part = lambda j: (0, j)
@@ -263,15 +255,14 @@
         grid=(cols // tile,),
         out_shape=jax.ShapeDtypeStruct((rows2, 128), jnp.float32),
         in_specs=[
-            pl.BlockSpec(g0.shape, whole),
-            pl.BlockSpec(g1.shape, whole),
+            pl.BlockSpec(g2.shape, lambda j: (0, 0, 0)),
             pl.BlockSpec((rows2, tile), part),
             pl.BlockSpec((p.shape[0], tile), part),
         ],
         out_specs=pl.BlockSpec((rows2, 128), whole),
         compiler_params=pltpu.CompilerParams(vmem_limit_bytes=GRANT),
         name="token_scores",
-    )(g0, g1, a2, p)
+    )(g2, a2, p)
 
 
 def finish_kernel(mp, t, out, send, recv):
@@ -329,23 +320,15 @@
     grads_own = rotate(train_grads, basis_out)
     query_block = rotate(query_acts, basis_in)
     query_grot = rotate(query_grads, basis_out)
-    acts2, grads_sib, query2, slot_sib = spread(mp, acts_block, grads_own, query_block, slot_rows)
+    acts2, grads2, query2, slot2, squared, total = spread(
+        mp, slots, acts_block, grads_own, grads_own.T, query_block, slot_rows
+    )
 
     own_first = core == 0
-    grads0 = jnp.where(own_first, grads_own, grads_sib)
-    grads1 = jnp.where(own_first, grads_sib, grads_own)
-    slot0 = jnp.where(own_first, slot_rows[0], slot_sib[0])
-    slot1 = jnp.where(own_first, slot_sib[0], slot_rows[0])
     names = jnp.arange(slots, dtype=jnp.float32)
-    mask0 = names[:, None] == slot0[None, :]
-    mask1 = names[:, None] == slot1[None, :]
-
-    def masked(grads, mask):
-        turned = grads.T
-        return jnp.where(mask[:, None, :], turned[None], jnp.zeros_like(turned)[None]).reshape(slots * width, rows)
-
-    squared, sums = squares(slots, masked(grads0, mask0), masked(grads1, mask1), acts2, tile)
-    total = jnp.broadcast_to(jnp.sum(sums), (8, 128))
+    mask0 = names[:, None] == slot2[0, 0][None, :]
+    mask1 = names[:, None] == slot2[1, 0][None, :]
+
     pieces, totals = scatter(n, mp, across, shape, squared, total)
 
     sequences = slots * dp
@@ -360,7 +343,7 @@
     precond = (local_grad / (curvature + damping)).astype(jnp.bfloat16)
     precond_full = collect(n, across, shape, (width, cols), precond)
 
-    by_token = jnp.sum(token_scores(grads0, grads1, acts2, precond_full, tile), axis=1)
+    by_token = jnp.sum(token_scores(grads2, acts2, precond_full, tile), axis=1)
     partial0 = jnp.sum(jnp.where(mask0, by_token[None, :rows], 0.0), axis=1)
     partial1 = jnp.sum(jnp.where(mask1, by_token[None, rows:], 0.0), axis=1)
     packed = jnp.zeros((8, 128), jnp.float32).at[0, :slots].set(partial0).at[1, :slots].set(partial1)

time: 203 us -> 187 us (0.921)
  other arithmetic: 16.5 us -> 7.14 us
  local copies, waits for them, and re-layouts: 9.67 us -> 4.3 us
  Pallas kernels: 161 us -> 158 us
    pallas_call x2 -> x1, Pallas kernels: 69.9 us -> 59.7 us  [spread(): pl.pallas_call(functools.partial(spread_kernel, mp, slots), out_shape=[ja...]
    select_n x4 -> x0, other arithmetic: 8.08 us -> none  [the longest x2 5.62 us: masked(): jnp.where(mask[:, None, :], turned[None], jnp.zeros_like(turned)[None])]
    pallas_call x1, Pallas kernels: 46.6 us -> 54.4 us  [scatter(): pl.pallas_call(functools.partial(scatter_kernel, n, mp, across, shape), o...]
    transpose x2 -> x0, local copies, waits for them, and re-layouts: 4.4 us -> none  [masked(): turned = grads.T]
    dot_general x4, matrix products: 12.1 us -> 14.7 us  [rotate(): jnp.dot(values, basis, preferred_element_type=jnp.float32)]
    convert_element_type x0 -> x1, local copies, waits for them, and re-layouts: none -> 2.16 us  [rotate(): jnp.dot(values, basis, preferred_element_type=jnp.float32)]
where the time goes in v2:
time: 187 us
  Pallas kernels  158 us (84%)
  matrix products  15.9 us (9%)
  other arithmetic  7.14 us (4%)
  local copies, waits for them, and re-layouts  4.3 us (2%)
    pallas_call x1, Pallas kernels, spread(): pl.pallas_call(functools.partial(spread_kernel, mp, slots), out_shape=[ja...  59.7 us
    pallas_call x1, Pallas kernels, scatter(): pl.pallas_call(functools.partial(scatter_kernel, n, mp, across, shape), o...  54.4 us
    pallas_call x1, Pallas kernels, collect(): pl.pallas_call(functools.partial(collect_kernel, n, across, shape), out_s...  26.6 us
    dot_general x4, matrix products, rotate(): jnp.dot(values, basis, preferred_element_type=jnp.float32)  14.7 us
    pallas_call x1, Pallas kernels, share(): pl.pallas_call(functools.partial(finish_kernel, mp), out_shape=jax.ShapeD...  11.3 us
    pallas_call x1, Pallas kernels, token_scores(): pl.pallas_call(score_kernel, grid=(cols // tile,), out_shape=jax.ShapeDty...  6.5 us

profile of v2, /device:TPU:0, one launch (start us, length us, event | category | flops | bytes accessed | tf_op | source)
XLA Modules:
  0.0 186.6 jit_solution(13729658249011525378)
XLA Ops:
  0.0 0.0 copy-start
  0.0 5.6 %convolution_convert_fusion = bf16[512,640]{0,1:T(8,128)(2,1)} fusion(bf16[512,2560]{1,0:T(8,128)(2,1)} %param.12, bf16[2560,640]{1,0:T(8,128)(2,1)} %param.17), kind=kOutput, calls=%fused_computation.3 | convolution fusion | flops 1678049280 | bytes 6553600 | tf_op jit(solution)/shard_map/dot_general | solution.py:17
  5.6 2.2 %copy.11.g = bf16[512,640]{1,0:T(8,128)(2,1)} copy(bf16[512,640]{0,1:T(8,128)(2,1)} %convolution_convert_fusion) | data formatting | bytes 1310720 | tf_op jit(solution)/shard_map/convert_element_type | solution.py:17
  7.8 0.0 copy-done
  7.8 0.0 copy-start.2
  7.8 4.9 %convolution_convert_fusion.1.a = bf16[512,640]{1,0:T(8,128)(2,1)} fusion(bf16[512,2560]{1,0:T(8,128)(2,1)} %param.11, bf16[2560,640]{1,0:T(8,128)(2,1)S(1)} %copy-done), kind=kOutput, calls=%fused_computation.4 | convolution fusion | flops 1678049280 | bytes 6553600 | tf_op jit(solution)/shard_map/dot_general | solution.py:17
  12.7 0.0 copy-done.2
  12.7 0.0 copy-start.5
  12.7 1.4 convolution_convert_fusion.2.q
  14.0 0.0 copy-done.5
  14.0 0.2 reduce-window.8
  14.2 0.1 convert_reduce_fusion.1
  14.3 0.6 broadcast_in_dim.31.s
  14.9 59.7 %spread.1 = (bf16[1024,1280]{1,0:T(8,128)(2,1)}, bf16[2,512,640]{2,1,0:T(8,128)(2,1)}, bf16[128,1280]{1,0:T(8,128)(2,1)}, f32[2,8,512]{2,1,0:T(8,128)}, bf16[640,1280]{1,0:T(8,128)(2,1)}, /*index=5*/f32[8,128]{1,0:T(8,128)}) custom-call(bf16[512,640]{1,0:T(8,128)(2,1)} %convolution_convert_fusion.1.a, bf16[512,640]{1,0:T(8,128)(2,1)} %copy.11.g, ...), custom_call_target="tpu_custom_call" | custom-call | tf_op jit(solution)/shard_map/spread/pallas_call | solution.py:115
  74.6 54.4 %scatter.13 = (bf16[4,160,1280]{2,1,0:T(8,128)(2,1)}, f32[4,8,8,128]{3,2,1,0:T(8,128)}) custom-call(bf16[640,1280]{1,0:T(8,128)(2,1)} %get-tuple-element.41.c, f32[8,128]{1,0:T(8,128)} %get-tuple-element.42.t), custom_call_target="tpu_custom_call" | custom-call | tf_op jit(solution)/shard_map/scatter/pallas_call | solution.py:188
  129.0 2.6 %convert_reduce_fusion = f32[160,1280]{1,0:T(8,128)} fusion(bf16[4,160,1280]{2,1,0:T(8,128)(2,1)} %get-tuple-element.43), kind=kLoop, calls=%fused_computation | loop fusion | flops 1433600 | bytes 2457600 | tf_op jit(solution)/shard_map/reduce_sum | solution.py:335
  131.6 1.5 slice_reduce_fusion
  133.8 0.0 copy-start.1
  133.8 0.0 copy-start.4
  133.8 2.9 %fusion.4 = bf16[128,640]{1,0:T(8,128)(2,1)S(1)} fusion(bf16[128,2560]{1,0:T(8,128)(2,1)} %param.15, bf16[2560,640]{1,0:T(8,128)(2,1)} %param.17), kind=kOutput, calls=%fused_computation.18 | convolution fusion | flops 419430400 | bytes 4096000 | tf_op jit(solution)/shard_map/dot_general | solution.py:17
  136.7 0.0 copy-done.1
  136.8 0.0 copy-done.4
  136.8 1.2 fusion.x
  137.9 26.6 %collect.1.p = bf16[640,1280]{1,0:T(8,128)(2,1)} custom-call(bf16[160,1280]{1,0:T(8,128)(2,1)} %fusion.x), custom_call_target="tpu_custom_call" | custom-call | tf_op jit(solution)/shard_map/collect/pallas_call | solution.py:222
  164.5 6.5 %token_scores.1 = f32[1024,128]{1,0:T(8,128)} custom-call(bf16[2,512,640]{2,1,0:T(8,128)(2,1)} %get-tuple-element.38.g2, bf16[1024,1280]{1,0:T(8,128)(2,1)} %get-tuple-element.39.a2, bf16[640,1280]{1,0:T(8,128)(2,1)} %collect.1.p), custom_call_target="tpu_custom_call" | custom-call | tf_op jit(solution)/shard_map/token_scores/pallas_call | solution.py:253
  171.0 1.2 reduce_sum.66
  172.3 0.7 fusion.2
  173.0 0.2 select_reduce_fusion
  173.2 0.2 scatter.12.t
  173.4 0.0 copy-start.3
  173.4 0.6 copy-done.3
  174.0 11.3 %share.1 = f32[8,8,128]{2,1,0:T(8,128)} custom-call(f32[8,128]{1,0:T(8,128)} %copy-done.3), custom_call_target="tpu_custom_call" | custom-call | tf_op jit(solution)/shard_map/share/pallas_call | solution.py:290
  185.3 0.8 reduce_sum.69
  186.0 0.5 broadcast_select_fusion
  (3 shorter events, 0.0 us)
Async XLA Ops:
  0.0 7.8 %copy-start = (bf16[2560,640]{1,0:T(8,128)(2,1)S(1)}, bf16[2560,640]{1,0:T(8,128)(2,1)}, u32[]{:S(2)}) copy-start(bf16[2560,640]{1,0:T(8,128)(2,1)} %param.16) | copy-start | bytes 9830404
  7.8 4.9 %copy-start.2 = (bf16[128,2560]{1,0:T(8,128)(2,1)S(1)}, bf16[128,2560]{1,0:T(8,128)(2,1)}, u32[]{:S(2)}) copy-start(bf16[128,2560]{1,0:T(8,128)(2,1)} %param.14) | copy-start | bytes 1966084
  12.7 1.4 copy-start.5
  133.8 2.9 %copy-start.1 = (f32[160,1280]{1,0:T(8,128)S(1)}, f32[160,1280]{1,0:T(8,128)}, u32[]{:S(2)}) copy-start(f32[160,1280]{1,0:T(8,128)} %convert_reduce_fusion) | copy-start | bytes 2457604
  133.8 2.9 %copy-start.4 = (bf16[128,1280]{1,0:T(8,128)(2,1)S(1)}, bf16[128,1280]{1,0:T(8,128)(2,1)}, u32[]{:S(2)}) copy-start(bf16[128,1280]{1,0:T(8,128)(2,1)} %get-tuple-element.40) | copy-start | bytes 983044
  173.4 0.6 copy-start.3
